TPU v7x, 32 devices: a whole 2x2x4 slice. The times are simulated.
32 devices in a mesh: grp: 2 (over y), dev: 16 (over z, x, core).
Axes of the slice: x: 2, y: 2, z: 4, core: 2. Of those that a mesh axis runs over, the one named last changes fastest.
Arguments:
- pooled_grad: bfloat16 [4096, 32, 128], P(('grp', 'dev')), may hold values from -6 to 6
- row_ids: int32 [4096, 4, 32], P(('grp', 'dev')), may hold values from 0 to 1023
- scale_exps: int32 [4096, 32], P(('grp', 'dev')), may hold values from 0 to 3
- table_owner: int32 [32], replicated, may hold values from 0 to 31, each once
- dense_acts: bfloat16 [4096, 512], P(('grp', 'dev')), may hold values from -6 to 6
- dense_cot: bfloat16 [4096, 512], P(('grp', 'dev')), may hold values from -0.1875 to 0.1875
Outputs:
- table_grad: float32 [32, 1024, 128], P('dev')
- weight_grad: float32 [512, 512], replicated
- bias_grad: float32 [512], replicated
Inputs may be any that keep to these rules, and one draw needn't show every extreme that they name: Table t's rows are accumulated into slot table_owner[t]; each slot belongs to exactly one table.
All inputs are finite; a program needn't handle non-finite values.
Results may differ from a plain program's by a relative error of at most 0.0003.
Values may be sent and summed in bfloat16 or wider, within the bound.
A program may use at most 128 MiB of HBM per device.

v0:
```python
import math

import jax
import jax.numpy as jnp
from jax import lax
from jax.sharding import PartitionSpec as P

ROWS = 1024


def powers(exps):
    return (
        1.0
        + (exps >= 1).astype(jnp.float32)
        + 2.0 * (exps >= 2).astype(jnp.float32)
        + 4.0 * (exps >= 3).astype(jnp.float32)
    )


def accumulate(grads, indices, exps):
    samples = grads.shape[0]
    slots = grads.shape[2]
    pool_len = indices.shape[3]
    block_rows = math.gcd(samples, 1024)
    row_axis = lax.broadcasted_iota(jnp.int32, (ROWS, 1), 0)
    results = []
    for slot_pos in range(slots):
        factor = powers(exps[:, 0, slot_pos])
        restored = (grads[:, 0, slot_pos, :].astype(jnp.float32) * factor[:, None]).astype(
            jnp.bfloat16
        )
        row_index = indices[:, 0, slot_pos, :]

        def add_block(count, running, restored=restored, row_index=row_index):
            offset = count * block_rows
            values = lax.dynamic_slice_in_dim(restored, offset, block_rows, 0)
            picked = lax.dynamic_slice_in_dim(row_index, offset, block_rows, 0)
            counts = jnp.zeros((ROWS, block_rows), jnp.float32)
            for lookup in range(pool_len):
                counts = counts + (picked[:, lookup][None, :] == row_axis).astype(jnp.float32)
            return running + jnp.dot(
                counts.astype(jnp.bfloat16), values, preferred_element_type=jnp.float32
            )

        start_grad = jnp.zeros((ROWS, grads.shape[3]), jnp.float32)
        results.append(lax.fori_loop(0, samples // block_rows, add_block, start_grad))
    return jnp.stack(results, 0)


def per_device(pooled_grad, row_ids, scale_exps, table_owner, dense_acts, dense_cot):
    batch_rows, tables, feat_width = pooled_grad.shape
    dev_count = lax.axis_size("dev")
    per_owner = tables // dev_count
    pool_len = row_ids.shape[1]
    factor = powers(scale_exps)
    quantized = jnp.clip(pooled_grad.astype(jnp.float32) / factor[:, :, None], -1.0, 1.0).astype(
        jnp.bfloat16
    )
    slot_table = (
        jnp.zeros((tables,), jnp.int32).at[table_owner].set(jnp.arange(tables, dtype=jnp.int32))
    )
    send_grads = jnp.take(quantized, slot_table, axis=1).reshape(
        batch_rows, dev_count, per_owner, feat_width
    )
    send_rows = jnp.transpose(
        jnp.take(row_ids, slot_table, axis=2).reshape(batch_rows, pool_len, dev_count, per_owner),
        (0, 2, 3, 1),
    )
    send_exps = jnp.take(scale_exps, slot_table, axis=1).reshape(batch_rows, dev_count, per_owner)
    weight_term = lax.dot_general(
        dense_acts, dense_cot, (((0,), (0,)), ((), ())), preferred_element_type=jnp.float32
    )
    bias_term = jnp.sum(dense_cot.astype(jnp.float32), axis=0)
    partial_grad = accumulate(
        lax.all_to_all(send_grads, "dev", split_axis=1, concat_axis=0, tiled=True),
        lax.all_to_all(send_rows, "dev", split_axis=1, concat_axis=0, tiled=True),
        lax.all_to_all(send_exps, "dev", split_axis=1, concat_axis=0, tiled=True),
    )
    table_grad = lax.psum(partial_grad, "grp")
    dense_parts = (
        lax.psum_scatter(weight_term, "dev", scatter_dimension=0, tiled=True),
        lax.psum_scatter(bias_term, "dev", scatter_dimension=0, tiled=True),
    )
    dense_parts = lax.psum((dense_parts[0], dense_parts[1]), "grp")
    weight_grad, bias_grad = (
        lax.all_gather(dense_parts[0], "dev", axis=0, tiled=True),
        lax.all_gather(dense_parts[1], "dev", axis=0, tiled=True),
    )
    return (table_grad, weight_grad, bias_grad)


def solution(mesh):
    return jax.shard_map(
        per_device,
        mesh=mesh,
        in_specs=(
            P(("grp", "dev"), None, None),
            P(("grp", "dev"), None, None),
            P(("grp", "dev"), None),
            P(),
            P(("grp", "dev"), None),
            P(("grp", "dev"), None),
        ),
        out_specs=(P("dev", None, None), P(), P()),
        check_vma=False,
    )
```

profile of v0, /device:TPU:0, one launch (start us, length us, event | category | flops | bytes accessed | tf_op | source)
XLA Modules:
  0.0 227.3 jit_solution(12590961035273388617)
XLA Ops:
  7.2 0.7 compare_select_fusion.5
  7.9 0.7 scatter_custom_fusion
  8.7 1.3 gather_fusion.2
  10.0 0.7 broadcast_select_fusion.1
  10.7 7.4 %all-to-all-start.2 = ((s32[128,16,2]{0,2,1:T(2,128)}), s32[128,16,2]{0,2,1:T(2,128)S(1)}, u32[]{:S(2)}, u32[]{:S(2)}) async-start(s32[128,16,2]{0,2,1:T(2,128)} %broadcast_select_fusion.1), calls=%async_computation.2 | async-start | bytes 32768 | tf_op jit(solution)/shard_map/all_to_all | solution.py:77
  18.1 0.7 select_add_fusion
  18.8 0.6 gather_fusion
  20.1 1.4 clamp_convert_fusion
  21.5 0.7 fusion.14
  22.2 0.7 gather_fusion.1
  23.0 1.7 all-to-all-done.2
  24.6 4.4 %all-to-all-start = ((s32[128,16,2,4]{0,2,3,1:T(2,128)}), s32[128,16,2,4]{0,2,3,1:T(2,128)S(1)}, u32[]{:S(2)}, u32[]{:S(2)}) async-start(s32[128,16,2,4]{0,2,3,1:T(2,128)} %fusion.14), calls=%async_computation | async-start | bytes 131072 | tf_op jit(solution)/shard_map/all_to_all | solution.py:76
  29.0 1.1 broadcast_select_fusion
  30.1 5.8 %all-to-all-done = s32[128,16,2,4]{0,2,3,1:T(2,128)S(1)} async-done(((s32[128,16,2,4]{0,2,3,1:T(2,128)}), s32[128,16,2,4]{0,2,3,1:T(2,128)S(1)}, u32[]{:S(2)}, u32[]{:S(2)}) %all-to-all-start) | async-done | bytes 65568 | tf_op jit(solution)/shard_map/all_to_all | solution.py:76
  35.9 3.7 %all-to-all-start.1 = ((bf16[128,16,2,128]{3,0,2,1:T(8,128)(2,1)}), bf16[128,16,2,128]{3,0,2,1:T(8,128)(2,1)S(1)}, u32[]{:S(2)}, u32[]{:S(2)}) async-start(bf16[128,16,2,128]{3,0,2,1:T(8,128)(2,1)} %broadcast_select_fusion), calls=%async_computation.1 | async-start | bytes 2097152 | tf_op jit(solution)/shard_map/all_to_all | solution.py:75
  39.6 1.3 fusion.25
  41.1 21.3 %all-to-all-done.1 = bf16[128,16,2,128]{3,0,2,1:T(8,128)(2,1)S(1)} async-done(((bf16[128,16,2,128]{3,0,2,1:T(8,128)(2,1)}), bf16[128,16,2,128]{3,0,2,1:T(8,128)(2,1)S(1)}, u32[]{:S(2)}, u32[]{:S(2)}) %all-to-all-start.1) | async-done | bytes 1048608 | tf_op jit(solution)/shard_map/all_to_all | solution.py:75
  62.5 0.7 fusion.13
  63.2 4.5 %while.31 = (s32[]{:T(128)}, f32[1024,128]{1,0:T(8,128)S(1)}, s32[2048,4]{0,1:T(4,128)S(1)}, bf16[2048,128]{1,0:T(8,128)(2,1)S(1)}, s32[]{:T(128)}, /*index=5*/s...) while((s32[]{:T(128)}, f32[1024,128]{1,0:T(8,128)S(1)}, ...), condition=%wide.region_4.5_spmd.clone.clone, body=%wide.region_3.4_spmd.clone.clone.sunk | while | flops 281280512 | bytes 1360101 | solution.py:46
  63.4 2.1 fusion.35
  65.6 2.1 fusion.35
  67.7 4.5 %while.30 = (s32[]{:T(128)}, f32[1024,128]{1,0:T(8,128)S(1)}, s32[2048,4]{0,1:T(4,128)S(1)}, bf16[2048,128]{1,0:T(8,128)(2,1)S(1)}, s32[]{:T(128)}, /*index=5*/s...) while((s32[]{:T(128)}, f32[1024,128]{1,0:T(8,128)S(1)}, ...), condition=%wide.region_2.3_spmd.clone.clone, body=%wide.region_1.2_spmd.clone.clone.sunk | while | flops 281280512 | bytes 1360101 | solution.py:46
  67.8 2.1 fusion.33
  70.1 2.1 fusion.33
  72.2 1.0 pad_maximum_fusion
  73.2 30.2 %reduce-scatter.2.cloned.1.call-done = f32[32,512]{1,0:T(8,128)} async-done(((f32[512,512]{1,0:T(8,128)}), f32[32,512]{1,0:T(8,128)}) %reduce-scatter.2.cloned.1.call-update) | async-done | bytes 65552 | tf_op jit(solution)/shard_map/reduce_scatter | solution.py:81
  103.5 43.5 %all-reduce.5.cloned.1.call-done = (f32[2,1024,128]{2,1,0:T(8,128)}, f32[32,512]{1,0:T(8,128)}) async-done(((f32[2,1024,128]{2,1,0:T(8,128)}, f32[32,512]{1,0:T(8,128)}), (f32[2,1024,128]{2,1,0:T(8,128)}, f32[32,512]{1,0:T(8,128)})) %all-reduce.5.cloned.1.call-update) | async-done | bytes 1114128 | tf_op jit(solution)/shard_map/psum | solution.py:79
  148.4 33.2 %all-reduce.1 = f32[512]{0:T(512)S(1)} all-reduce(f32[512]{0:T(512)S(1)} %convert_reduce_fusion), channel_id=3, replica_groups=mesh['grp'=2,'dev'=16] {'dev'}, use_global_device_ids=true, to_apply=%region_9.10.clone | all-reduce | flops 512 | bytes 4096
  182.3 4.9 %psum.23 = f32[32]{0:T(128)S(1)} all-reduce(f32[32]{0:T(128)S(1)} %dynamic-slice.2), channel_id=1, replica_groups=mesh['grp'=2,'dev'=16] {'grp'}, use_global_device_ids=true, to_apply=%region_10.11 | all-reduce | flops 32 | bytes 256 | tf_op jit(solution)/shard_map/psum | solution.py:84
  187.4 30.0 %all-reduce = f32[512]{0:T(512)} all-reduce(f32[512]{0:T(512)S(1)} %dynamic-update-slice), channel_id=1, replica_groups=mesh['grp'=2,'dev'=16] {'dev'}, use_global_device_ids=true, to_apply=%add | all-reduce | flops 512 | bytes 4096
  217.5 2.4 %copy.52 = f32[2,1024,128]{2,1,0:T(8,128)} copy(f32[2,1024,128]{2,1,0:T(8,128)} %get-tuple-element.448) | data formatting | bytes 2097152
  219.8 1.0 copy.53
  (41 shorter events, 2.4 us)
Async XLA Ops:
  7.2 32.4 %copy-start = (bf16[128,512]{1,0:T(8,128)(2,1)S(1)}, bf16[128,512]{1,0:T(8,128)(2,1)}, u32[]{:S(2)}) copy-start(bf16[128,512]{1,0:T(8,128)(2,1)} %param.14) | copy-start | bytes 393220
  7.2 11.7 %copy-start.1 = (s32[128,4,32]{0,2,1:T(8,128)S(1)}, s32[128,4,32]{0,2,1:T(8,128)}, u32[]{:S(2)}) copy-start(s32[128,4,32]{0,2,1:T(8,128)} %param.11) | copy-start | bytes 196612
  10.7 13.9 %all-to-all-start.2 = ((s32[128,16,2]{0,2,1:T(2,128)}), s32[128,16,2]{0,2,1:T(2,128)S(1)}, u32[]{:S(2)}, u32[]{:S(2)}) async-start(s32[128,16,2]{0,2,1:T(2,128)} %broadcast_select_fusion.1), calls=%async_computation.2 | async-start | bytes 32768 | tf_op jit(solution)/shard_map/all_to_all | solution.py:77
  18.8 1.2 copy-start.2
  24.6 11.3 %all-to-all-start = ((s32[128,16,2,4]{0,2,3,1:T(2,128)}), s32[128,16,2,4]{0,2,3,1:T(2,128)S(1)}, u32[]{:S(2)}, u32[]{:S(2)}) async-start(s32[128,16,2,4]{0,2,3,1:T(2,128)} %fusion.14), calls=%async_computation | async-start | bytes 131072 | tf_op jit(solution)/shard_map/all_to_all | solution.py:76
  30.1 9.5 %copy-start.4 = (bf16[128,512]{1,0:T(8,128)(2,1)S(1)}, bf16[128,512]{1,0:T(8,128)(2,1)}, u32[]{:S(2)}) copy-start(bf16[128,512]{1,0:T(8,128)(2,1)} %param.15) | copy-start | bytes 393220
  35.9 26.5 %all-to-all-start.1 = ((bf16[128,16,2,128]{3,0,2,1:T(8,128)(2,1)}), bf16[128,16,2,128]{3,0,2,1:T(8,128)(2,1)S(1)}, u32[]{:S(2)}, u32[]{:S(2)}) async-start(bf16[128,16,2,128]{3,0,2,1:T(8,128)(2,1)} %broadcast_select_fusion), calls=%async_computation.1 | async-start | bytes 2097152 | tf_op jit(solution)/shard_map/all_to_all | solution.py:75
  39.5 63.9 %reduce-scatter.2.cloned.1.call-start = ((), (), s32[]{:S(2)}) async-start(), calls=%async_computation.4 | async-start | bytes 1114112 | tf_op jit(solution)/shard_map/reduce_scatter | solution.py:81
  40.9 106.1 %all-reduce.5.cloned.1.call-start = ((), (), s32[]{:S(2)}) async-start(), calls=%async_computation.6 | async-start | bytes 2228224 | tf_op jit(solution)/shard_map/psum | solution.py:79
  73.2 73.9 %copy-start.5 = (u32[32]{0:T(128)S(1)}, u32[32]{0:T(128)}, u32[]{:S(2)}) copy-start(u32[32]{0:T(128)} %constant.132) | copy-start | bytes 388
  103.5 114.0 %all-gather.2.cloned.1.call-start = ((), (), s32[]{:S(2)}) async-start(), calls=%async_computation.5 | async-start | bytes 1114112 | tf_op jit(solution)/shard_map/all_gather | solution.py:86
  217.5 2.4 %copy-start.3 = (f32[512,512]{1,0:T(8,128)S(1)}, f32[512,512]{1,0:T(8,128)}, u32[]{:S(2)}) copy-start(f32[512,512]{1,0:T(8,128)} %all-gather.2.cloned.1.call-done) | copy-start | bytes 3145732
Sparse Core Ops, SparseCore 0:
  44.6 58.8 reduce-scatter.1
  106.4 40.5 all-reduce.4
  149.2 37.8 all-gather.1
where the time goes:
time: 228 us; the launch traced here: 227 us
  waiting for transfers between devices  102 us (45%)
  blocking collectives  68.2 us (30%)
  starting transfers between devices  15.5 us (7%)
  between operations  15.3 us (7%)
  matrix products  9.65 us (4%)
  local copies, waits for them, and re-layouts  8.8 us (4%)
  other arithmetic  7.24 us (3%)
    unnamed x2, blocking collectives  63.2 us
    psum x1, waiting for transfers between devices, per_device(): table_grad = lax.psum(partial_grad, 'grp')  43.5 us
    reduce_scatter x1, waiting for transfers between devices, per_device(): lax.psum_scatter(weight_term, 'dev', scatter_dimension=0, tiled=True)  30.2 us
    all_to_all x1, waiting for transfers between devices, per_device(): lax.all_to_all(send_grads, 'dev', split_axis=1, concat_axis=0, tiled=True)  21.3 us
    dot_general x4, matrix products, add_block(): jnp.dot(counts.astype(jnp.bfloat16), values, preferred_element_type=jnp.f...  8.36 us
    all_to_all x1, starting transfers between devices, per_device(): lax.all_to_all(send_exps, 'dev', split_axis=1, concat_axis=0, tiled=True)  7.39 us
    all_to_all x1, waiting for transfers between devices, per_device(): lax.all_to_all(send_rows, 'dev', split_axis=1, concat_axis=0, tiled=True)  5.76 us
    psum x1, blocking collectives, per_device(): dense_parts = lax.psum((dense_parts[0], dense_parts[1]), 'grp')  4.93 us
  transfers between devices with their start and end apart: 6, of which 5 were waited for; matrix products, arithmetic and copies ran while one was open for 8% of the time, Pallas kernels for 0%

commit v1 on v0

v1 whole, which is shorter than its diff:
```python
import functools

import jax
import jax.numpy as jnp
from jax import lax
from jax.experimental import pallas as pl
from jax.experimental.pallas import tpu as pltpu
from jax.sharding import PartitionSpec as P

ROWS = 1024
DIGIT = 32
MESH = pl.DeviceIdType.MESH
ROW_BLOCK = 256


def powers(exps):
    return (
        1.0
        + (exps >= 1).astype(jnp.float32)
        + 2.0 * (exps >= 2).astype(jnp.float32)
        + 4.0 * (exps >= 3).astype(jnp.float32)
    )


def kernel(
    devs,
    pool,
    slot_ref,
    x_ref,
    ids_ref,
    acts_ref,
    cot_ref,
    table_ref,
    weight_ref,
    bias_ref,
    send,
    recv,
    part,
    whole,
    half0,
    half1,
    half2,
    zbuf,
    bpart,
    bhalf,
    bz,
    asend,
    arecv,
    fsend,
    frecv,
    dsend,
    drecv,
    esend,
    erecv,
    zsend,
    zrecv,
    bsend,
    brecv,
    gsend,
    grecv,
):
    me = lax.axis_index("dev")
    grp = lax.axis_index("grp")
    other = 1 - grp
    owned, samples, feat = table_ref.shape[0], x_ref.shape[1], x_ref.shape[2]
    id_rows = ids_ref.shape[1]
    zs = devs // 4
    core = lax.rem(me, 2)
    xbit = lax.rem(lax.div(me, 2), 2)
    z = lax.div(me, 4)
    hid, hid2 = weight_ref.shape
    wide = hid2 // 128
    total = hid * wide

    def remote(src, dst, ssem, rsem, dev, group):
        return pltpu.make_async_remote_copy(
            src_ref=src,
            dst_ref=dst,
            send_sem=ssem,
            recv_sem=rsem,
            device_id={"grp": group, "dev": dev},
            device_id_type=MESH,
        )

    for j in range(wide):
        part[pl.ds(j * hid, hid), :] = lax.dot_general(
            acts_ref[...],
            cot_ref[:, j * 128 : (j + 1) * 128],
            (((0,), (0,)), ((), ())),
            preferred_element_type=jnp.float32,
        )
    bpart[0] = jnp.zeros(bpart.shape[1:], jnp.float32)
    for j in range(wide):
        bpart[0, j : j + 1, :] = jnp.sum(
            cot_ref[:, j * 128 : (j + 1) * 128].astype(jnp.float32), axis=0, keepdims=True
        )

    near = me + 1 - 2 * core
    across = me + 2 - 4 * xbit
    stages = (
        (near, grp, core, half0),
        (across, grp, xbit, half1),
        (me, other, grp, half2),
    )
    bases = [0]
    for s in range(3):
        size = total >> (s + 1)
        bases.append(bases[s] + stages[s][2] * size)

    def halving(s):
        dev, group, bit, landing = stages[s]
        size = total >> (s + 1)
        away = pl.multiple_of(bases[s] + (1 - bit) * size, 8)
        return (
            remote(
                part.at[pl.ds(away, size)], landing, dsend.at[s], drecv.at[s], dev, group
            ),
            remote(bpart.at[s], bhalf.at[s], bsend.at[s], brecv.at[s], dev, group),
        )

    def halving_start(s):
        for copy in halving(s):
            copy.start()

    def halving_finish(s):
        for copy in halving(s):
            copy.wait()
        size = total >> (s + 1)
        keep = pl.multiple_of(bases[s + 1], 8)
        part[pl.ds(keep, size), :] = part[pl.ds(keep, size), :] + stages[s][3][...]
        bpart[s + 1] = bpart[s] + bhalf[s]

    piece = (total >> 3) // zs

    def z_copy(k):
        peer = lax.rem(z + k, zs)
        dev = peer * 4 + lax.rem(me, 4)
        away = pl.multiple_of(bases[3] + peer * piece, 8)
        return (
            remote(
                part.at[pl.ds(away, piece)], zbuf.at[z], zsend.at[peer], zrecv.at[z], dev, grp
            ),
            remote(bpart.at[3], bz.at[z], bsend.at[3 + peer], brecv.at[3 + z], dev, grp),
        )

    def z_wait(k):
        peer = lax.rem(z + k, zs)
        dev = peer * 4 + lax.rem(me, 4)
        here = pl.multiple_of(bases[3] + z * piece, 8)
        return (
            remote(
                part.at[pl.ds(here, piece)], zbuf.at[peer], zsend.at[peer], zrecv.at[peer], dev, grp
            ),
            remote(bpart.at[3], bz.at[peer], bsend.at[3 + peer], brecv.at[3 + peer], dev, grp),
        )

    mine = pl.multiple_of(bases[3] + z * piece, 8)

    def z_start():
        @pl.loop(1, zs)
        def _(k):
            for copy in z_copy(k):
                copy.start()

    def z_finish():
        zbuf[z] = part[pl.ds(mine, piece), :]
        bz[z] = bpart[3]

        @pl.loop(1, zs)
        def _(k):
            for copy in z_wait(k):
                copy.wait_recv()

        @pl.loop(1, zs)
        def _(k):
            for copy in z_copy(k):
                copy.wait_send()

        whole[pl.ds(mine, piece), :] = lax.fori_loop(
            1, zs, lambda i, run: run + zbuf[i], zbuf[0]
        )
        bsum = lax.fori_loop(1, zs, lambda i, run: run + bz[i], bz[0])
        for j in range(wide):
            bias_ref[:, j * 128 : (j + 1) * 128] = bsum[j : j + 1, :]

    def zg_copy(k, back):
        peer = lax.rem(z + k, zs)
        dev = peer * 4 + lax.rem(me, 4)
        off = mine if not back else pl.multiple_of(bases[3] + peer * piece, 8)
        block = whole.at[pl.ds(off, piece)]
        return remote(block, block, gsend.at[peer], grecv.at[peer if back else z], dev, grp)

    def zg_start():
        @pl.loop(1, zs)
        def _(k):
            zg_copy(k, False).start()

    def zg_finish():
        @pl.loop(1, zs)
        def _(k):
            zg_copy(k, True).wait_recv()

        @pl.loop(1, zs)
        def _(k):
            zg_copy(k, False).wait_send()

    def doubling(s, back):
        dev, group, bit, _ = stages[s]
        size = total >> (s + 1)
        off = bases[s] + (1 - bit) * size if back else bases[s + 1]
        block = whole.at[pl.ds(pl.multiple_of(off, 8), size)]
        return remote(block, block, esend.at[s], erecv.at[s], dev, group)

    def doubling_start(s):
        doubling(s, False).start()

    def doubling_finish(s):
        doubling(s, True).wait_recv()
        doubling(s, False).wait_send()

    halving_start(0)

    def chunk_copy(k):
        dst = lax.rem(me + k, devs)
        return remote(
            send.at[dst], recv.at[0, me], asend.at[dst], arecv.at[me], dst, grp
        )

    def arrival(k):
        src = lax.rem(me - k + devs, devs)
        return remote(
            send.at[src], recv.at[0, src], asend.at[src], arecv.at[src], src, grp
        )

    def forward(k):
        src = lax.rem(me - k + devs, devs)
        return remote(
            recv.at[0, src], recv.at[1, src], fsend.at[src], frecv.at[src], me, other
        )

    def build(k):
        dst = lax.rem(me + k, devs)
        digits = []
        for s in range(owned):
            t = slot_ref[dst * owned + s]
            send[dst, pl.ds(s * samples, samples), :] = x_ref[t]
            digits.append(ids_ref[t])
        send[dst, pl.ds(owned * samples, owned * id_rows), :] = jnp.concatenate(
            digits, axis=0
        ).astype(jnp.bfloat16)

    build(0)
    recv[0, me] = send[me]

    @pl.loop(1, devs)
    def _(k):
        build(k)
        chunk_copy(k).start()

    forward(0).start()
    table_ref[...] = jnp.zeros(table_ref.shape, jnp.float32)

    def accumulate(side, j):
        first = lax.rem(me - 2 * j + devs, devs)
        second = lax.rem(me - 2 * j - 1 + devs, devs)
        digits = jnp.concatenate(
            [
                recv[side, c, pl.ds(owned * samples, owned * id_rows), :].astype(jnp.float32)
                for c in (first, second)
            ],
            axis=1,
        )
        for s in range(owned):
            top = digits[s * id_rows : s * id_rows + pool]
            low = digits[s * id_rows + pool : s * id_rows + 2 * pool]
            rows = top * DIGIT + low
            values = jnp.concatenate(
                [recv[side, c, pl.ds(s * samples, samples), :] for c in (first, second)],
                axis=0,
            )
            for block in range(ROWS // ROW_BLOCK):
                local = rows - block * ROW_BLOCK
                local = jnp.where((local >= 0) & (local < ROW_BLOCK), local, -1.0).astype(
                    jnp.bfloat16
                )
                axis = lax.broadcasted_iota(
                    jnp.int32, (ROW_BLOCK, 2 * samples), 0
                ).astype(jnp.float32).astype(jnp.bfloat16)
                one, zero = jnp.bfloat16(1), jnp.bfloat16(0)
                counts = jnp.where(local[0:1] == axis, one, zero)
                for p in range(1, pool):
                    counts = counts + jnp.where(local[p : p + 1] == axis, one, zero)
                span = pl.ds(block * ROW_BLOCK, ROW_BLOCK)
                table_ref[s, span, :] = table_ref[s, span, :] + jnp.dot(
                    counts, values, preferred_element_type=jnp.float32
                )

    pairs = devs // 2
    cuts = [0, pairs // 4, pairs // 2, 3 * pairs // 4, pairs]

    def own_loop(seg):
        @pl.loop(cuts[seg], cuts[seg + 1])
        def _(j):
            for k in (2 * j, 2 * j + 1):

                @pl.when(k > 0)
                def _(k=k):
                    arrival(k).wait_recv()
                    forward(k).start()

            accumulate(0, j)

    def far_loop(seg):
        @pl.loop(cuts[seg], cuts[seg + 1])
        def _(j):
            for k in (2 * j, 2 * j + 1):
                src = lax.rem(me - k + devs, devs)
                remote(
                    recv.at[0, src], recv.at[1, src], fsend.at[src], frecv.at[src], me, other
                ).wait_recv()
            accumulate(1, j)

    halving_finish(0)
    halving_start(1)
    own_loop(0)
    halving_finish(1)
    halving_start(2)
    own_loop(1)
    halving_finish(2)
    z_start()
    own_loop(2)
    z_finish()
    zg_start()
    own_loop(3)
    zg_finish()
    doubling_start(2)
    far_loop(0)
    doubling_finish(2)
    doubling_start(1)
    far_loop(1)
    far_loop(2)
    doubling_finish(1)
    doubling_start(0)
    far_loop(3)
    doubling_finish(0)
    for j in range(wide):
        weight_ref[:, j * 128 : (j + 1) * 128] = whole[pl.ds(j * hid, hid), :]

    @pl.loop(1, devs)
    def _(k):
        chunk_copy(k).wait_send()

    @pl.loop(0, devs)
    def _(k):
        forward(k).wait_send()


def solution(mesh):
    devs = mesh.shape["dev"]

    def per_device(pooled_grad, row_ids, scale_exps, table_owner, dense_acts, dense_cot):
        samples, tables, feat = pooled_grad.shape
        pool = row_ids.shape[1]
        owned = tables // devs
        hid, hid2 = dense_acts.shape[1], dense_cot.shape[1]
        zs = devs // 4
        factor = powers(scale_exps)[:, :, None]
        restored = jnp.transpose(
            jnp.clip(pooled_grad.astype(jnp.float32), -factor, factor).astype(jnp.bfloat16),
            (1, 0, 2),
        )
        by_table = jnp.transpose(row_ids, (2, 1, 0))
        digits = jnp.concatenate([by_table // DIGIT, by_table % DIGIT], axis=1).astype(jnp.float32)
        order = jnp.arange(tables, dtype=jnp.int32)
        slots = jnp.sum(
            jnp.where(table_owner[None, :] == order[:, None], order[None, :], 0), axis=1
        ).astype(jnp.int32)
        rows = owned * samples + owned * digits.shape[1]
        total = hid * hid2 // 128
        dma = pltpu.SemaphoreType.DMA
        vmem = pl.BlockSpec(memory_space=pltpu.VMEM)
        table_grad, weight_grad, bias_grad = pl.pallas_call(
            functools.partial(kernel, devs, pool),
            out_shape=(
                jax.ShapeDtypeStruct((owned, ROWS, feat), jnp.float32),
                jax.ShapeDtypeStruct((hid, hid2), jnp.float32),
                jax.ShapeDtypeStruct((1, hid2), jnp.float32),
            ),
            in_specs=[pl.BlockSpec(memory_space=pltpu.SMEM)] + [vmem] * 4,
            out_specs=(vmem, vmem, vmem),
            scratch_shapes=[
                pltpu.VMEM((devs, rows, feat), jnp.bfloat16),
                pltpu.VMEM((2, devs, rows, feat), jnp.bfloat16),
                pltpu.VMEM((total, 128), jnp.float32),
                pltpu.VMEM((total, 128), jnp.float32),
                pltpu.VMEM((total // 2, 128), jnp.float32),
                pltpu.VMEM((total // 4, 128), jnp.float32),
                pltpu.VMEM((total // 8, 128), jnp.float32),
                pltpu.VMEM((zs, total // 8 // zs, 128), jnp.float32),
                pltpu.VMEM((4, 8, 128), jnp.float32),
                pltpu.VMEM((3, 8, 128), jnp.float32),
                pltpu.VMEM((zs, 8, 128), jnp.float32),
                dma((devs,)),
                dma((devs,)),
                dma((devs,)),
                dma((devs,)),
                dma((3,)),
                dma((3,)),
                dma((3,)),
                dma((3,)),
                dma((zs,)),
                dma((zs,)),
                dma((3 + zs,)),
                dma((3 + zs,)),
                dma((zs,)),
                dma((zs,)),
            ],
            compiler_params=pltpu.CompilerParams(has_side_effects=True),
        )(slots, restored, digits, dense_acts, dense_cot)
        return table_grad, weight_grad, bias_grad.reshape(hid2)

    return jax.shard_map(
        per_device,
        mesh=mesh,
        in_specs=(
            P(("grp", "dev"), None, None),
            P(("grp", "dev"), None, None),
            P(("grp", "dev"), None),
            P(),
            P(("grp", "dev"), None),
            P(("grp", "dev"), None),
        ),
        out_specs=(P("dev", None, None), P(), P()),
        check_vma=False,
    )
```

time: 228 us -> 76.5 us (0.34)
  waiting for transfers between devices: 102 us -> 0 us
  blocking collectives: 68.2 us -> 0 us
  Pallas kernels: 0 us -> 63.9 us
  starting transfers between devices: 15.5 us -> 0 us
  between operations: 15.3 us -> 0.65 us
  matrix products: 9.65 us -> 0 us
  local copies, waits for them, and re-layouts: 8.8 us -> 3.91 us
    pallas_call x0 -> x1, Pallas kernels: none -> 63.9 us  [per_device(): pl.pallas_call(functools.partial(kernel, devs, pool), out_shape=(jax.Shap...]
    unnamed x2 -> x0, blocking collectives: 63.2 us -> none
    psum x1 -> x0, waiting for transfers between devices: 43.5 us -> none  [per_device(): table_grad = lax.psum(partial_grad, 'grp')]
    reduce_scatter x1 -> x0, waiting for transfers between devices: 30.2 us -> none  [per_device(): lax.psum_scatter(weight_term, 'dev', scatter_dimension=0, tiled=True)]
    all_to_all x3 -> x0, waiting for transfers between devices: 28.7 us -> none  [the longest x1 21.3 us: per_device(): lax.all_to_all(send_grads, 'dev', split_axis=1, concat_axis=0, tiled=True)]
    all_to_all x3 -> x0, starting transfers between devices: 15.4 us -> none  [the longest x1 7.39 us: per_device(): lax.all_to_all(send_exps, 'dev', split_axis=1, concat_axis=0, tiled=True)]
    dot_general x5 -> x0, matrix products: 9.65 us -> none  [the longest x4 8.36 us: add_block(): jnp.dot(counts.astype(jnp.bfloat16), values, preferred_element_type=jnp.f...]
    psum x1 -> x0, blocking collectives: 4.93 us -> none  [per_device(): dense_parts = lax.psum((dense_parts[0], dense_parts[1]), 'grp')]
  transfers between devices with their start and end apart: 6 -> 0, of which waited for: 5 -> 0; matrix products, arithmetic and copies ran while one was open for 8% -> 0% of each run, Pallas kernels for 0% -> 0%
where the time goes in v1:
time: 76.5 us; the launch traced here: 75.1 us
  Pallas kernels  63.9 us (84%)
  other arithmetic  6.73 us (9%)
  local copies, waits for them, and re-layouts  3.91 us (5%)
    pallas_call x1, Pallas kernels, per_device(): pl.pallas_call(functools.partial(kernel, devs, pool), out_shape=(jax.Shap...  63.9 us
    unnamed x7, local copies, waits for them, and re-layouts  3.91 us
    transpose x1, other arithmetic, per_device(): jnp.transpose(jnp.clip(pooled_grad.astype(jnp.float32), -factor, factor)....  3.07 us

profile of v1, /device:TPU:0, one launch (start us, length us, event | category | flops | bytes accessed | tf_op | source)
XLA Modules:
  0.0 75.1 jit_solution(1735678174254721717)
XLA Ops:
  0.6 1.3 %select_reduce_fusion.slot_ref = s32[32]{0:T(128)} fusion(s32[32]{0:T(128)} %param.9), kind=kLoop, calls=%fused_computation.14 | loop fusion | flops 3040 | bytes 256 | tf_op jit(solution)/shard_map/reduce_sum | solution.py:375
  1.9 0.7 select_add_fusion
  2.6 1.0 %add_select_fusion.1 = (s32[32,4,128]{2,1,0:T(4,128)S(1)}, s32[32,4,128]{2,1,0:T(4,128)S(1)}) fusion(s32[128,4,32]{0,2,1:T(8,128)} %param.7), kind=kLoop, calls=%fused_computation.4 | loop fusion | flops 311296 | bytes 196608 | tf_op jit(solution)/shard_map/jit(floor_divide)/jit(_where)/select_n | solution.py:373
  3.6 0.7 add_convert_fusion.ids_ref
  4.3 3.1 %fusion.x_ref = bf16[32,128,128]{2,1,0:T(8,128)(2,1)} fusion(bf16[128,32,128]{2,1,0:T(8,128)(2,1)} %param.6, bf16[128,32]{0,1:T(8,128)(2,1)S(1)} %get-tuple-element.12, bf16[128,32]{0,1:T(8,128)(2,1)S(1)} %get-tuple-element.11), kind=kLoop, calls=%fused_computation.1 | loop fusion | flops 3145728 | bytes 2113536 | tf_op jit(solution)/shard_map/transpose | solution.py:368
  7.4 63.9 %shard_map.85 = (f32[2,1024,128]{2,1,0:T(8,128)}, f32[512,512]{1,0:T(8,128)}, f32[1,512]{1,0:T(1,128)}) custom-call(s32[32]{0:T(128)} %select_reduce_fusion.slot_ref, bf16[32,128,128]{2,1,0:T(8,128)(2,1)} %fusion.x_ref, f32[32,8,128]{2,1,0:T(8,128)} %add_convert_fusion.ids_ref, bf16[128,512]{1,0:T(8,128)(2,1)} %acts_ref.1, bf16[128,512]{1,0:T(8,128)(2,1)} %cot_ref.1), custom_call_target="tpu_custom_call" | custom-call | tf_op jit(solution)/shard_map/pallas_call | solution.py:382
  71.2 0.0 copy-start
  71.2 2.4 %copy.32 = f32[2,1024,128]{2,1,0:T(8,128)} copy(f32[2,1024,128]{2,1,0:T(8,128)} %get-tuple-element.16) | data formatting | bytes 2097152
  73.6 0.0 copy-done
  73.6 0.0 copy-start.1
  73.6 1.0 %copy.33 = f32[512,512]{1,0:T(8,128)} copy(f32[512,512]{1,0:T(8,128)S(1)} %copy-done) | data formatting | bytes 2097152
  74.6 0.0 copy-done.1
  74.6 0.6 copy.34
Async XLA Ops:
  71.2 2.4 %copy-start = (f32[512,512]{1,0:T(8,128)S(1)}, f32[512,512]{1,0:T(8,128)}, u32[]{:S(2)}) copy-start(f32[512,512]{1,0:T(8,128)} %get-tuple-element.17) | copy-start | bytes 3145732
  73.6 1.0 %copy-start.1 = (f32[1,512]{1,0:T(1,128)S(1)}, f32[1,512]{1,0:T(1,128)}, u32[]{:S(2)}) copy-start(f32[1,512]{1,0:T(1,128)} %get-tuple-element.8) | copy-start | bytes 6148

commit v2 on v1

--- a/solution.py
+++ b/solution.py
@@ -8,7 +8,8 @@
 from jax.sharding import PartitionSpec as P
 
 ROWS = 1024
-DIGIT = 32
+DIGIT_BITS = 5
+DIGIT = 1 << DIGIT_BITS
 MESH = pl.DeviceIdType.MESH
 ROW_BLOCK = 256
 
@@ -35,6 +36,7 @@
     bias_ref,
     send,
     recv,
+    inter,
     part,
     whole,
     half0,
@@ -44,8 +46,10 @@
     bpart,
     bhalf,
     bz,
-    asend,
-    arecv,
+    psend,
+    precv,
+    csend,
+    crecv,
     fsend,
     frecv,
     dsend,
@@ -63,7 +67,7 @@
     grp = lax.axis_index("grp")
     other = 1 - grp
     owned, samples, feat = table_ref.shape[0], x_ref.shape[1], x_ref.shape[2]
-    id_rows = ids_ref.shape[1]
+    id_rows = 2 * ids_ref.shape[1]
     zs = devs // 4
     core = lax.rem(me, 2)
     xbit = lax.rem(lax.div(me, 2), 2)
@@ -82,18 +86,19 @@
             device_id_type=MESH,
         )
 
-    for j in range(wide):
-        part[pl.ds(j * hid, hid), :] = lax.dot_general(
-            acts_ref[...],
-            cot_ref[:, j * 128 : (j + 1) * 128],
-            (((0,), (0,)), ((), ())),
-            preferred_element_type=jnp.float32,
-        )
-    bpart[0] = jnp.zeros(bpart.shape[1:], jnp.float32)
-    for j in range(wide):
-        bpart[0, j : j + 1, :] = jnp.sum(
-            cot_ref[:, j * 128 : (j + 1) * 128].astype(jnp.float32), axis=0, keepdims=True
-        )
+    def dense_partial():
+        for j in range(wide):
+            part[pl.ds(j * hid, hid), :] = lax.dot_general(
+                acts_ref[...],
+                cot_ref[:, j * 128 : (j + 1) * 128],
+                (((0,), (0,)), ((), ())),
+                preferred_element_type=jnp.float32,
+            )
+        bpart[0] = jnp.zeros(bpart.shape[1:], jnp.float32)
+        for j in range(wide):
+            bpart[0, j : j + 1, :] = jnp.sum(
+                cot_ref[:, j * 128 : (j + 1) * 128].astype(jnp.float32), axis=0, keepdims=True
+            )
 
     near = me + 1 - 2 * core
     across = me + 2 - 4 * xbit
@@ -218,51 +223,119 @@
         doubling(s, True).wait_recv()
         doubling(s, False).wait_send()
 
-    halving_start(0)
-
-    def chunk_copy(k):
-        dst = lax.rem(me + k, devs)
+    place = lax.rem(me, 4)
+    places = (
+        place,
+        place + 1 - 2 * core,
+        place + 2 - 4 * xbit,
+        place + 3 - 4 * xbit - 2 * core,
+    )
+
+    barrier = pltpu.get_barrier_semaphore()
+
+    def greet(dev, group):
+        pl.semaphore_signal(
+            barrier, inc=1, device_id={"grp": group, "dev": dev}, device_id_type=MESH
+        )
+
+    for m in range(1, 4):
+        greet(z * 4 + places[m], grp)
+
+    @pl.loop(1, zs)
+    def _(k):
+        greet(lax.rem(z + k, zs) * 4 + place, grp)
+
+    greet(me, other)
+    pl.semaphore_wait(barrier, 3 + zs)
+
+    def each_far(act):
+        @pl.loop(1, zs)
+        def _(i):
+            for peer in (z + zs - i, z - zs + i):
+                pl.when((peer >= 0) & (peer < zs))(functools.partial(act, peer))
+
+    def each_near(act):
+        @pl.loop(1, zs)
+        def _(i):
+            for peer in (z + i, z - i):
+                pl.when((peer >= 0) & (peer < zs))(functools.partial(act, peer))
+
+    def column_copy(m, peer):
         return remote(
-            send.at[dst], recv.at[0, me], asend.at[dst], arecv.at[me], dst, grp
-        )
-
-    def arrival(k):
-        src = lax.rem(me - k + devs, devs)
+            send.at[peer * 4 + places[m]],
+            inter.at[m - 1, peer],
+            psend.at[m - 1, peer],
+            precv.at[m - 1, peer],
+            z * 4 + places[m],
+            grp,
+        )
+
+    def level_copy(m, back=False):
+        who = z * 4 + places[m]
         return remote(
-            send.at[src], recv.at[0, src], asend.at[src], arecv.at[src], src, grp
-        )
-
-    def forward(k):
-        src = lax.rem(me - k + devs, devs)
+            send.at[who],
+            recv.at[0, who if back else me],
+            psend.at[m - 1, z],
+            precv.at[m - 1, z],
+            who,
+            grp,
+        )
+
+    def line_copy(m, peer):
+        origin = send.at[peer * 4 + place] if m == 0 else inter.at[m - 1, peer]
+        return remote(
+            origin,
+            recv.at[0, z * 4 + places[m]],
+            csend.at[m, peer],
+            crecv.at[m, z],
+            peer * 4 + place,
+            grp,
+        )
+
+    def line_wait(m, peer):
+        landing = recv.at[0, peer * 4 + places[m]]
+        remote(
+            landing, landing, csend.at[m, peer], crecv.at[m, peer], peer * 4 + place, grp
+        ).wait_recv()
+
+    def forward(src):
         return remote(
             recv.at[0, src], recv.at[1, src], fsend.at[src], frecv.at[src], me, other
         )
 
-    def build(k):
-        dst = lax.rem(me + k, devs)
+    def build(dst):
         digits = []
         for s in range(owned):
             t = slot_ref[dst * owned + s]
             send[dst, pl.ds(s * samples, samples), :] = x_ref[t]
-            digits.append(ids_ref[t])
+            picked = ids_ref[t]
+            digits += [picked >> DIGIT_BITS, picked & (DIGIT - 1)]
         send[dst, pl.ds(owned * samples, owned * id_rows), :] = jnp.concatenate(
             digits, axis=0
-        ).astype(jnp.bfloat16)
-
-    build(0)
+        ).astype(jnp.float32).astype(jnp.bfloat16)
+
+    pl.loop(0, devs)(build)
     recv[0, me] = send[me]
 
-    @pl.loop(1, devs)
-    def _(k):
-        build(k)
-        chunk_copy(k).start()
-
-    forward(0).start()
-    table_ref[...] = jnp.zeros(table_ref.shape, jnp.float32)
-
-    def accumulate(side, j):
-        first = lax.rem(me - 2 * j + devs, devs)
-        second = lax.rem(me - 2 * j - 1 + devs, devs)
+    def column_start(m):
+        each_far(lambda peer: column_copy(m, peer).start())
+        level_copy(m).start()
+
+    def column_pass(m):
+        def act(peer):
+            column_copy(m, peer).wait_recv()
+            line_copy(m, peer).start()
+
+        each_far(act)
+        level_copy(m, True).wait_recv()
+        forward(z * 4 + places[m]).start()
+
+    each_far(lambda peer: line_copy(0, peer).start())
+    column_start(2)
+    column_start(1)
+    forward(me).start()
+
+    def accumulate(side, first, second):
         digits = jnp.concatenate(
             [
                 recv[side, c, pl.ds(owned * samples, owned * id_rows), :].astype(jnp.float32)
@@ -295,64 +368,73 @@
                     counts, values, preferred_element_type=jnp.float32
                 )
 
-    pairs = devs // 2
-    cuts = [0, pairs // 4, pairs // 2, 3 * pairs // 4, pairs]
-
-    def own_loop(seg):
-        @pl.loop(cuts[seg], cuts[seg + 1])
-        def _(j):
-            for k in (2 * j, 2 * j + 1):
-
-                @pl.when(k > 0)
-                def _(k=k):
-                    arrival(k).wait_recv()
-                    forward(k).start()
-
-            accumulate(0, j)
-
-    def far_loop(seg):
-        @pl.loop(cuts[seg], cuts[seg + 1])
-        def _(j):
-            for k in (2 * j, 2 * j + 1):
-                src = lax.rem(me - k + devs, devs)
-                remote(
-                    recv.at[0, src], recv.at[1, src], fsend.at[src], frecv.at[src], me, other
-                ).wait_recv()
-            accumulate(1, j)
-
+    def pair(side, half, peer):
+        accumulate(side, peer * 4 + places[2 * half], peer * 4 + places[2 * half + 1])
+
+    def line_pass(m):
+        def act(peer):
+            line_wait(m, peer)
+            forward(peer * 4 + places[m]).start()
+
+        each_near(act)
+
+    def own_pairs(half):
+        pair(0, half, z)
+        each_near(functools.partial(pair, 0, half))
+
+    def far_pair(half, peer):
+        for m in (2 * half, 2 * half + 1):
+            forward(peer * 4 + places[m]).wait_recv()
+        pair(1, half, peer)
+
+    dense_partial()
+    halving_start(0)
+    column_pass(1)
+    table_ref[...] = jnp.zeros(table_ref.shape, jnp.float32)
     halving_finish(0)
     halving_start(1)
-    own_loop(0)
+    column_start(3)
+    column_pass(2)
+    line_pass(0)
     halving_finish(1)
     halving_start(2)
-    own_loop(1)
+    line_pass(1)
     halving_finish(2)
     z_start()
-    own_loop(2)
+    column_pass(3)
+    own_pairs(0)
+    line_pass(2)
     z_finish()
     zg_start()
-    own_loop(3)
+    far_pair(0, z)
+    line_pass(3)
     zg_finish()
     doubling_start(2)
-    far_loop(0)
+    own_pairs(1)
+    each_near(functools.partial(far_pair, 0))
     doubling_finish(2)
     doubling_start(1)
-    far_loop(1)
-    far_loop(2)
+    far_pair(1, z)
+    each_near(functools.partial(far_pair, 1))
     doubling_finish(1)
     doubling_start(0)
-    far_loop(3)
     doubling_finish(0)
     for j in range(wide):
         weight_ref[:, j * 128 : (j + 1) * 128] = whole[pl.ds(j * hid, hid), :]
 
-    @pl.loop(1, devs)
-    def _(k):
-        chunk_copy(k).wait_send()
+    def drain(peer):
+        for m in range(4):
+            line_copy(m, peer).wait_send()
+            if m > 0:
+                column_copy(m, peer).wait_send()
+
+    each_near(drain)
+    for m in range(1, 4):
+        level_copy(m).wait_send()
 
     @pl.loop(0, devs)
-    def _(k):
-        forward(k).wait_send()
+    def _(src):
+        forward(src).wait_send()
 
 
 def solution(mesh):
@@ -370,12 +452,11 @@
             (1, 0, 2),
         )
         by_table = jnp.transpose(row_ids, (2, 1, 0))
-        digits = jnp.concatenate([by_table // DIGIT, by_table % DIGIT], axis=1).astype(jnp.float32)
         order = jnp.arange(tables, dtype=jnp.int32)
         slots = jnp.sum(
             jnp.where(table_owner[None, :] == order[:, None], order[None, :], 0), axis=1
         ).astype(jnp.int32)
-        rows = owned * samples + owned * digits.shape[1]
+        rows = owned * samples + owned * 2 * pool
         total = hid * hid2 // 128
         dma = pltpu.SemaphoreType.DMA
         vmem = pl.BlockSpec(memory_space=pltpu.VMEM)
@@ -391,6 +472,7 @@
             scratch_shapes=[
                 pltpu.VMEM((devs, rows, feat), jnp.bfloat16),
                 pltpu.VMEM((2, devs, rows, feat), jnp.bfloat16),
+                pltpu.VMEM((3, zs, rows, feat), jnp.bfloat16),
                 pltpu.VMEM((total, 128), jnp.float32),
                 pltpu.VMEM((total, 128), jnp.float32),
                 pltpu.VMEM((total // 2, 128), jnp.float32),
@@ -400,8 +482,10 @@
                 pltpu.VMEM((4, 8, 128), jnp.float32),
                 pltpu.VMEM((3, 8, 128), jnp.float32),
                 pltpu.VMEM((zs, 8, 128), jnp.float32),
-                dma((devs,)),
-                dma((devs,)),
+                dma((3, zs)),
+                dma((3, zs)),
+                dma((4, zs)),
+                dma((4, zs)),
                 dma((devs,)),
                 dma((devs,)),
                 dma((3,)),
@@ -415,8 +499,8 @@
                 dma((zs,)),
                 dma((zs,)),
             ],
-            compiler_params=pltpu.CompilerParams(has_side_effects=True),
-        )(slots, restored, digits, dense_acts, dense_cot)
+            compiler_params=pltpu.CompilerParams(collective_id=0, has_side_effects=True),
+        )(slots, restored, by_table, dense_acts, dense_cot)
         return table_grad, weight_grad, bias_grad.reshape(hid2)
 
     return jax.shard_map(

time: 76.5 us -> 64.5 us (0.84); the launches traced: 75.1 us -> 64.2 us
  Pallas kernels: 63.9 us -> 53 us
  other arithmetic: 6.73 us -> 5.08 us
  local copies, waits for them, and re-layouts: 3.91 us -> 5.42 us
    pallas_call x1, Pallas kernels: 63.9 us -> 53 us  [per_device(): pl.pallas_call(functools.partial(kernel, devs, pool), out_shape=(jax.Shap...]
    unnamed x7 -> x8, local copies, waits for them, and re-layouts: 3.91 us -> 5.42 us
    select_n x1 -> x0, other arithmetic: 0.97 us -> none  [per_device(): by_table // DIGIT]
where the time goes in v2:
time: 64.5 us; the launch traced here: 64.2 us
  Pallas kernels  53 us (82%)
  local copies, waits for them, and re-layouts  5.42 us (8%)
  other arithmetic  5.08 us (8%)
  between operations  0.65 us (1%)
    pallas_call x1, Pallas kernels, per_device(): pl.pallas_call(functools.partial(kernel, devs, pool), out_shape=(jax.Shap...  53 us
    unnamed x8, local copies, waits for them, and re-layouts  5.42 us
    transpose x1, other arithmetic, per_device(): jnp.transpose(jnp.clip(pooled_grad.astype(jnp.float32), -factor, factor)....  3.07 us

profile of v2, /device:TPU:0, one launch (start us, length us, event | category | flops | bytes accessed | tf_op | source)
XLA Modules:
  0.0 64.2 jit_solution(4113493788717400083)
XLA Ops:
  0.6 1.3 %select_reduce_fusion.slot_ref = s32[32]{0:T(128)} fusion(s32[32]{0:T(128)} %param.9), kind=kLoop, calls=%fused_computation.4 | loop fusion | flops 3040 | bytes 256 | tf_op jit(solution)/shard_map/reduce_sum | solution.py:456
  1.9 0.7 %select_add_fusion = (bf16[128,32]{0,1:T(8,128)(2,1)S(1)}, bf16[128,32]{0,1:T(8,128)(2,1)S(1)}) fusion(s32[128,32]{0,1:T(8,128)} %param.8), kind=kLoop, calls=%fused_computation.3 | loop fusion | flops 53248 | bytes 32768 | tf_op jit(solution)/shard_map/add | solution.py:19
  2.6 1.5 %copy.15 = s32[128,4,32]{0,1,2:T(4,128)} copy(s32[128,4,32]{0,2,1:T(8,128)} %param.7) | data formatting | bytes 131072 | tf_op args[1]
  4.2 3.1 %fusion.x_ref = bf16[32,128,128]{2,1,0:T(8,128)(2,1)} fusion(bf16[128,32,128]{2,1,0:T(8,128)(2,1)} %param.6, bf16[128,32]{0,1:T(8,128)(2,1)S(1)} %get-tuple-element.10, bf16[128,32]{0,1:T(8,128)(2,1)S(1)} %get-tuple-element.9), kind=kLoop, calls=%fused_computation.1 | loop fusion | flops 3145728 | bytes 2113536 | tf_op jit(solution)/shard_map/transpose | solution.py:450
  7.2 53.0 %shard_map.85 = (f32[2,1024,128]{2,1,0:T(8,128)}, f32[512,512]{1,0:T(8,128)}, f32[1,512]{1,0:T(1,128)}) custom-call(s32[32]{0:T(128)} %select_reduce_fusion.slot_ref, bf16[32,128,128]{2,1,0:T(8,128)(2,1)} %fusion.x_ref, s32[32,4,128]{2,1,0:T(4,128)} %bitcast.6, bf16[128,512]{1,0:T(8,128)(2,1)} %acts_ref.1, bf16[128,512]{1,0:T(8,128)(2,1)} %cot_ref.1), custom_call_target="tpu_custom_call" | custom-call | tf_op jit(solution)/shard_map/pallas_call | solution.py:463
  60.3 0.0 copy-start
  60.3 2.4 %copy.19 = f32[2,1024,128]{2,1,0:T(8,128)} copy(f32[2,1024,128]{2,1,0:T(8,128)} %get-tuple-element.14) | data formatting | bytes 2097152
  62.6 0.0 copy-done
  62.6 0.0 copy-start.1
  62.6 1.0 %copy.20 = f32[512,512]{1,0:T(8,128)} copy(f32[512,512]{1,0:T(8,128)S(1)} %copy-done) | data formatting | bytes 2097152
  63.6 0.0 copy-done.1
  63.6 0.6 copy.21
Async XLA Ops:
  60.3 2.4 %copy-start = (f32[512,512]{1,0:T(8,128)S(1)}, f32[512,512]{1,0:T(8,128)}, u32[]{:S(2)}) copy-start(f32[512,512]{1,0:T(8,128)} %get-tuple-element.15) | copy-start | bytes 3145732
  62.6 1.0 %copy-start.1 = (f32[1,512]{1,0:T(1,128)S(1)}, f32[1,512]{1,0:T(1,128)}, u32[]{:S(2)}) copy-start(f32[1,512]{1,0:T(1,128)} %get-tuple-element.8) | copy-start | bytes 6148
